TPU v7x, 128 devices: a whole 4x4x4 slice. The times are simulated.
128 devices in a mesh: prob: 1, samp: 2 (over core), feat: 64 (over z, y, x).
Axes of the slice: x: 4, y: 4, z: 4, core: 2. Of those that a mesh axis runs over, the one named last changes fastest.
Arguments:
- x_mat: bfloat16 [8192, 65536], P(('prob', 'samp'), 'feat')
- w_init: float32 [65536, 64], P(('prob', 'feat'))
- targets: float32 [8192, 64], P(('prob', 'samp'))
- step_size: float32 [65536], P(('prob', 'feat'))
Outputs:
- output 1: float32 [65536, 64], P(('prob', 'feat'))
- output 2: float32 [8192, 64], P(('prob', 'samp'))
All inputs are finite; a program needn't handle non-finite values.
Results may differ from a plain program's by a relative error of at most 0.00316278.
Values are sent between devices in bfloat16 or wider.
A program may use at most 1 GiB of HBM per device.

v0:
```python
import jax
import jax.numpy as jnp
from jax import lax
from jax.sharding import PartitionSpec as P, NamedSharding

SWEEPS = 4
COMBINE_WEIGHT = 0.8
RIDGE_SCALE = 0.1


def solution(mesh):
    samp_count = mesh.shape["samp"]
    feat_count = mesh.shape["feat"]

    def local_solve(x_loc, w_loc, y_loc, eta_loc):
        rows_loc, feat_len = x_loc.shape
        samples = rows_loc * samp_count
        ridge = RIDGE_SCALE * (feat_len * feat_count) / samples
        first = jnp.dot(x_loc, w_loc.astype(jnp.bfloat16), preferred_element_type=jnp.float32)
        residual = y_loc - lax.psum(first.astype(jnp.bfloat16).astype(jnp.float32), "feat")
        weights = w_loc
        for sweep in range(SWEEPS):
            part_grad = lax.dot_general(x_loc, residual.astype(jnp.bfloat16), (((0,), (0,)), ((), ())), preferred_element_type=jnp.float32)
            gradient = lax.psum(part_grad, "samp") / samples
            delta = eta_loc[:, None] * (gradient - ridge * weights)
            weights = weights + COMBINE_WEIGHT * delta
            update = jnp.dot(x_loc, delta.astype(jnp.bfloat16), preferred_element_type=jnp.float32)
            residual = residual - COMBINE_WEIGHT * lax.psum(update.astype(jnp.bfloat16).astype(jnp.float32), "feat")
        return weights, residual

    return jax.shard_map(
        local_solve,
        mesh=mesh,
        in_specs=(P(("prob", "samp"), "feat"), P(("prob", "feat"), None), P(("prob", "samp"), None), P(("prob", "feat"))),
        out_specs=(P(("prob", "feat"), None), P(("prob", "samp"), None)),
        check_vma=False,
    )
```

profile of v0, /device:TPU:1, one launch (start us, length us, event | category | flops | bytes accessed | tf_op | source)
XLA Modules:
  0.0 827.2 jit_solution(14518582877050481651)
XLA Ops:
  7.2 0.0 copy-start.6
  7.2 0.0 all-reduce.10.cloned.1.call-start
  7.2 7.1 fusion.8
  14.3 0.0 all-reduce.10.cloned.1.call-update
  14.3 0.0 all-reduce.12.cloned.1.call-start
  14.4 132.8 %all-reduce.10.cloned.1.call-done = f32[4096,64]{0,1:T(8,128)} async-done(((f32[4096,64]{0,1:T(8,128)}), f32[4096,64]{0,1:T(8,128)}) %all-reduce.10.cloned.1.call-update) | async-done | bytes 1048592 | tf_op jit(solution)/shard_map/psum | solution.py:20
  147.2 0.0 copy-done.6
  147.2 1.3 sub.27
  148.6 0.0 copy-start
  148.6 0.0 copy-start.9
  148.6 5.7 convolution_bitcast_fusion.3
  154.3 0.0 all-reduce.12.cloned.1.call-update
  154.3 0.0 all-reduce.14.cloned.1.call-start
  154.4 23.4 %all-reduce.12.cloned.1.call-done = f32[1024,64]{0,1:T(8,128)} async-done(((f32[1024,64]{0,1:T(8,128)}), f32[1024,64]{0,1:T(8,128)}) %all-reduce.12.cloned.1.call-update) | async-done | bytes 262160 | tf_op jit(solution)/shard_map/psum | solution.py:24
  177.7 0.0 copy-done
  177.7 7.1 fusion.7
  184.8 0.0 all-reduce.14.cloned.1.call-update
  184.9 0.0 all-reduce.16.cloned.1.call-start
  184.9 130.6 %all-reduce.14.cloned.1.call-done = f32[4096,64]{0,1:T(8,128)} async-done(((f32[4096,64]{0,1:T(8,128)}), f32[4096,64]{0,1:T(8,128)}) %all-reduce.14.cloned.1.call-update) | async-done | bytes 1048592 | tf_op jit(solution)/shard_map/psum | solution.py:28
  315.5 6.0 convolution_bitcast_fusion.2
  321.5 0.0 all-reduce.16.cloned.1.call-update
  321.5 0.0 all-reduce.18.cloned.1.call-start
  321.6 23.4 %all-reduce.16.cloned.1.call-done = f32[1024,64]{0,1:T(8,128)} async-done(((f32[1024,64]{0,1:T(8,128)}), f32[1024,64]{0,1:T(8,128)}) %all-reduce.16.cloned.1.call-update) | async-done | bytes 262160 | tf_op jit(solution)/shard_map/psum | solution.py:24
  344.9 0.0 copy-done.3
  344.9 7.1 fusion.5
  352.1 0.0 all-reduce.18.cloned.1.call-update
  352.1 0.0 all-reduce.20.cloned.1.call-start
  352.1 130.6 %all-reduce.18.cloned.1.call-done = f32[4096,64]{0,1:T(8,128)} async-done(((f32[4096,64]{0,1:T(8,128)}), f32[4096,64]{0,1:T(8,128)}) %all-reduce.18.cloned.1.call-update) | async-done | bytes 1048592 | tf_op jit(solution)/shard_map/psum | solution.py:28
  482.7 1.4 multiply_subtract_fusion.2
  484.2 5.7 convolution_bitcast_fusion.1
  489.9 0.0 all-reduce.20.cloned.1.call-update
  489.9 0.2 all-reduce.22.cloned.1.call-start
  490.1 0.1 multiply_add_fusion.2
  490.3 23.0 %all-reduce.20.cloned.1.call-done = f32[1024,64]{0,1:T(8,128)} async-done(((f32[1024,64]{0,1:T(8,128)}), f32[1024,64]{0,1:T(8,128)}) %all-reduce.20.cloned.1.call-update) | async-done | bytes 262160 | tf_op jit(solution)/shard_map/psum | solution.py:24
  513.3 7.1 fusion.3
  520.4 0.0 all-reduce.22.cloned.1.call-update
  520.4 0.0 all-reduce.24.cloned.1.call-start
  520.5 130.6 %all-reduce.22.cloned.1.call-done = f32[4096,64]{0,1:T(8,128)} async-done(((f32[4096,64]{0,1:T(8,128)}), f32[4096,64]{0,1:T(8,128)}) %all-reduce.22.cloned.1.call-update) | async-done | bytes 1048592 | tf_op jit(solution)/shard_map/psum | solution.py:28
  651.1 6.0 convolution_bitcast_fusion
  657.1 0.0 all-reduce.24.cloned.1.call-update
  657.1 0.0 all-reduce.26.cloned.1.call-start
  657.2 23.4 %all-reduce.24.cloned.1.call-done = f32[1024,64]{0,1:T(8,128)} async-done(((f32[1024,64]{0,1:T(8,128)}), f32[1024,64]{0,1:T(8,128)}) %all-reduce.24.cloned.1.call-update) | async-done | bytes 262160 | tf_op jit(solution)/shard_map/psum | solution.py:24
  680.5 7.1 fusion.1
  687.7 0.0 all-reduce.26.cloned.1.call-update
  687.7 0.8 multiply_add_fusion
  688.5 129.8 %all-reduce.26.cloned.1.call-done = f32[4096,64]{0,1:T(8,128)} async-done(((f32[4096,64]{0,1:T(8,128)}), f32[4096,64]{0,1:T(8,128)}) %all-reduce.26.cloned.1.call-update) | async-done | bytes 1048592 | tf_op jit(solution)/shard_map/psum | solution.py:28
  818.3 0.0 copy-done.1
  818.3 2.4 multiply_subtract_fusion
  (13 shorter events, 0.0 us)
Async XLA Ops:
  7.2 140.1 %copy-start.6 = (f32[4096,64]{0,1:T(8,128)S(1)}, f32[4096,64]{0,1:T(8,128)}, u32[]{:S(2)}) copy-start(f32[4096,64]{0,1:T(8,128)} %param.6) | copy-start | bytes 3145732
  7.2 140.0 %all-reduce.10.cloned.1.call-start = ((), (), s32[]{:S(2)}) async-start(), calls=%async_computation | async-start | bytes 2097152 | tf_op jit(solution)/shard_map/psum | solution.py:20
  14.3 163.4 %all-reduce.12.cloned.1.call-start = ((), (), s32[]{:S(2)}) async-start(), calls=%async_computation.1 | async-start | bytes 524288 | tf_op jit(solution)/shard_map/psum | solution.py:24
  148.6 29.2 %copy-start = (f32[1024,64]{0,1:T(8,128)S(1)}, f32[1024,64]{0,1:T(8,128)}, u32[]{:S(2)}) copy-start(f32[1024,64]{0,1:T(8,128)} %param.5) | copy-start | bytes 786436
  148.6 29.2 %copy-start.9 = (f32[1024]{0:T(1024)S(1)}, f32[1024]{0:T(1024)}, u32[]{:S(2)}) copy-start(f32[1024]{0:T(1024)} %param.7) | copy-start | bytes 12292
  154.3 161.2 %all-reduce.14.cloned.1.call-start = ((), (), s32[]{:S(2)}) async-start(), calls=%async_computation.2 | async-start | bytes 2097152 | tf_op jit(solution)/shard_map/psum | solution.py:28
  184.8 160.1 %copy-start.3 = (f32[1024,64]{0,1:T(8,128)S(1)}, f32[1024,64]{0,1:T(8,128)}, u32[]{:S(2)}) copy-start(f32[1024,64]{0,1:T(8,128)} %all-reduce.12.cloned.1.call-done) | copy-start | bytes 786436
  184.9 160.1 %all-reduce.16.cloned.1.call-start = ((), (), s32[]{:S(2)}) async-start(), calls=%async_computation.3 | async-start | bytes 524288 | tf_op jit(solution)/shard_map/psum | solution.py:24
  321.5 161.2 %copy-start.2 = (f32[4096,64]{0,1:T(8,128)S(1)}, f32[4096,64]{0,1:T(8,128)}, u32[]{:S(2)}) copy-start(f32[4096,64]{0,1:T(8,128)} %all-reduce.14.cloned.1.call-done) | copy-start | bytes 3145732
  321.5 161.2 %all-reduce.18.cloned.1.call-start = ((), (), s32[]{:S(2)}) async-start(), calls=%async_computation.4 | async-start | bytes 2097152 | tf_op jit(solution)/shard_map/psum | solution.py:28
  352.1 161.2 %all-reduce.20.cloned.1.call-start = ((), (), s32[]{:S(2)}) async-start(), calls=%async_computation.5 | async-start | bytes 524288 | tf_op jit(solution)/shard_map/psum | solution.py:24
  484.1 6.0 copy-start.4
  484.1 6.0 copy-start.7
  489.9 161.2 %all-reduce.22.cloned.1.call-start = ((), (), s32[]{:S(2)}) async-start(), calls=%async_computation.6 | async-start | bytes 2097152 | tf_op jit(solution)/shard_map/psum | solution.py:28
  520.4 160.1 %copy-start.5 = (f32[1024,64]{0,1:T(8,128)S(1)}, f32[1024,64]{0,1:T(8,128)}, u32[]{:S(2)}) copy-start(f32[1024,64]{0,1:T(8,128)} %all-reduce.20.cloned.1.call-done) | copy-start | bytes 786436
  520.4 160.1 %all-reduce.24.cloned.1.call-start = ((), (), s32[]{:S(2)}) async-start(), calls=%async_computation.7 | async-start | bytes 524288 | tf_op jit(solution)/shard_map/psum | solution.py:24
  657.1 161.2 %copy-start.1 = (f32[4096,64]{0,1:T(8,128)S(1)}, f32[4096,64]{0,1:T(8,128)}, u32[]{:S(2)}) copy-start(f32[4096,64]{0,1:T(8,128)} %all-reduce.22.cloned.1.call-done) | copy-start | bytes 3145732
  657.1 161.2 %all-reduce.26.cloned.1.call-start = ((), (), s32[]{:S(2)}) async-start(), calls=%async_computation.8 | async-start | bytes 2097152 | tf_op jit(solution)/shard_map/psum | solution.py:28
  680.5 7.2 copy-start.8
Sparse Core Ops, SparseCore 0:
  14.5 132.7 all-reduce.9
  154.4 23.2 all-reduce.11
  185.0 130.4 all-reduce.13
  321.6 23.2 all-reduce.15
  352.2 130.4 all-reduce.17
  490.0 23.2 all-reduce.19
  520.6 130.4 all-reduce.21
  657.2 23.2 all-reduce.23
  687.8 130.4 all-reduce.25
where the time goes:
time: 829 us; the launch traced here: 827 us
  waiting for transfers between devices  748 us (90%)
  matrix products  59 us (7%)
  between operations  13.9 us (2%)
    psum x4, waiting for transfers between devices, local_solve(): lax.psum(update.astype(jnp.bfloat16).astype(jnp.float32), 'feat')  522 us
    psum x1, waiting for transfers between devices, local_solve(): lax.psum(first.astype(jnp.bfloat16).astype(jnp.float32), 'feat')  133 us
    psum x4, waiting for transfers between devices, local_solve(): gradient = lax.psum(part_grad, 'samp') / samples  93.1 us
    dot_general x4, matrix products, local_solve(): jnp.dot(x_loc, delta.astype(jnp.bfloat16), preferred_element_type=jnp.flo...  28.5 us
    dot_general x4, matrix products, local_solve(): lax.dot_general(x_loc, residual.astype(jnp.bfloat16), (((0,), (0,)), ((),...  23.4 us
  transfers between devices with their start and end apart: 9, of which 9 were waited for; matrix products, arithmetic and copies ran while one was open for 0% of the time, Pallas kernels for 0%

commit v1 on v0

v1 whole, which is shorter than its diff:
```python
import jax
import jax.numpy as jnp
from jax import lax
from jax.experimental import pallas as pl
from jax.experimental.pallas import tpu as pltpu
from jax.sharding import PartitionSpec as P

SWEEPS = 4
COMBINE_WEIGHT = 0.8
RIDGE_SCALE = 0.1
SIDE = 4
MESH_ID = pl.DeviceIdType.MESH

PLANE = sorted(
    [(dx, dy) for dy in range(SIDE) for dx in range(SIDE)],
    key=lambda d: -(min(d[0], SIDE - d[0]) + min(d[1], SIDE - d[1])),
)
FAR_FIRST = (2, 1, 3, 0)
NEAR_FIRST = (0, 1, 3, 2)


def solution(mesh):
    samp_count = mesh.shape["samp"]
    feat_count = mesh.shape["feat"]
    assert feat_count == SIDE**3 and samp_count == 2

    def make_kernel(rows, feat_len, targets, ridge, samples):
        half = rows // 2
        chunk = half // feat_count
        plane = half // SIDE
        lanes = 2 * targets
        f32, bf16 = jnp.float32, jnp.bfloat16

        def kernel(x_hbm, w_hbm, y_hbm, eta_ref, wt_out, rp_out, x_v, w_v, y_v, ub, rs, rb, rown, rf, wt, gacc, gx, wl, wr,
                   x_sem, in_sem, rs_send, rs_recv, ag_send, ag_recv, gx_send, gx_recv, out_sem):
            samp = lax.axis_index("samp")
            me = lax.axis_index("feat")
            cx, cy, cz = me % SIDE, (me // SIDE) % SIDE, me // (SIDE * SIDE)
            nx = [(cx + d) % SIDE for d in range(SIDE)]
            ny = [((cy + d) % SIDE) * SIDE for d in range(SIDE)]
            nz = [(cz + d) % SIDE for d in range(SIDE)]
            sibling = (0, 1 - samp, me)

            def peer_of(dx, dy, dz):
                return nz[dz] * (SIDE * SIDE) + ny[dy] + nx[dx]

            def rows_of(index):
                return pl.ds(pl.multiple_of(index * chunk, chunk), chunk)

            w_copy = pltpu.make_async_copy(w_hbm, w_v, in_sem.at[0])
            w_copy.start()
            x_copies = []
            for order, dz in enumerate(FAR_FIRST):
                pair = []
                for side in range(2):
                    block = pl.ds(pl.multiple_of(side * half + nz[dz] * plane, plane), plane)
                    pair.append(pltpu.make_async_copy(x_hbm.at[block], x_v.at[block], x_sem.at[2 * order + side]))
                    pair[-1].start()
                x_copies.append(pair)
            y_copies = []
            for side in range(2):
                block = pl.ds(pl.multiple_of(side * half + me * chunk, chunk), chunk)
                y_copies.append(pltpu.make_async_copy(y_hbm.at[block], y_v.at[side], in_sem.at[1 + side]))
                y_copies[-1].start()

            barrier = pltpu.get_barrier_semaphore()
            pl.semaphore_signal(barrier, inc=1, device_id=sibling, device_id_type=MESH_ID)
            for dz in FAR_FIRST:
                for dx, dy in PLANE:
                    if (dx, dy, dz) != (0, 0, 0):
                        pl.semaphore_signal(barrier, inc=1, device_id=(0, samp, peer_of(dx, dy, dz)), device_id_type=MESH_ID)

            w_copy.wait()
            start = w_v[...]
            zero = jnp.zeros((feat_len, targets), bf16)
            wl[...] = jnp.concatenate([start.astype(bf16), zero], axis=1)
            wr[...] = jnp.concatenate([zero, start.astype(bf16)], axis=1)
            for col in range(feat_len // 128):
                wt[:, col * 128:(col + 1) * 128] = jnp.transpose(start[col * 128:(col + 1) * 128, :])
            for copy in y_copies:
                copy.wait()
            rown[...] = jnp.concatenate([y_v[0], y_v[1]], axis=1)

            def send_terms(before):
                for order, dz in enumerate(FAR_FIRST):
                    before(order)
                    left = pl.ds(pl.multiple_of(nz[dz] * plane, plane), plane)
                    right = pl.ds(pl.multiple_of(half + nz[dz] * plane, plane), plane)
                    term = jnp.dot(x_v[left, :], wl[...], preferred_element_type=f32)
                    term += jnp.dot(x_v[right, :], wr[...], preferred_element_type=f32)
                    ub[left, :] = term.astype(bf16)
                    for dx, dy in PLANE:
                        if (dx, dy, dz) == (0, 0, 0):
                            continue
                        peer = peer_of(dx, dy, dz)
                        pltpu.make_async_remote_copy(
                            src_ref=ub.at[rows_of(peer)], dst_ref=rs.at[rows_of(me)], send_sem=rs_send, recv_sem=rs_recv.at[dz],
                            device_id=(0, samp, peer), device_id_type=MESH_ID).start()
                rs[rows_of(me), :] = ub[rows_of(me), :]

            def wait_rows(ref, count, sem):
                block = ref.at[pl.ds(0, count)]
                pltpu.make_async_copy(block, block, sem).wait()

            def group(dz):
                return plane - chunk if dz == 0 else plane

            def reduce_terms(scale):
                for dz in NEAR_FIRST:
                    wait_rows(rs, group(dz), rs_recv.at[dz])
                total = rs[0:chunk, :].astype(f32)
                for index in range(1, feat_count):
                    total += rs[index * chunk:(index + 1) * chunk, :].astype(f32)
                rown[...] = rown[...] - scale * total

            def send_owned(src, dst):
                for dz in FAR_FIRST:
                    for dx, dy in PLANE:
                        if (dx, dy, dz) == (0, 0, 0):
                            continue
                        pltpu.make_async_remote_copy(
                            src_ref=src, dst_ref=dst.at[rows_of(me)], send_sem=ag_send, recv_sem=ag_recv.at[dz],
                            device_id=(0, samp, peer_of(dx, dy, dz)), device_id_type=MESH_ID).start()

            def from_plane(dz):
                return nz[(SIDE - dz) % SIDE]

            def sweep(step, unused):
                def before(order):
                    @pl.when(step == 0)
                    def _():
                        for copy in x_copies[order]:
                            copy.wait()
                        if order == 0:
                            pl.semaphore_wait(barrier, feat_count)

                send_terms(before)
                reduce_terms(jnp.where(step == 0, 1.0, COMBINE_WEIGHT))
                rb[rows_of(me), :] = rown[...].astype(bf16)
                send_owned(rb.at[rows_of(me)], rb)
                for place, dz in enumerate(NEAR_FIRST):
                    wait_rows(rb, group(dz), ag_recv.at[dz])
                    source = from_plane(dz)
                    left = pl.ds(pl.multiple_of(source * plane, plane), plane)
                    right = pl.ds(pl.multiple_of(half + source * plane, plane), plane)
                    turned = jnp.transpose(rb[left, :])
                    grad = jnp.dot(turned[:targets], x_v[left, :], preferred_element_type=f32)
                    grad += jnp.dot(turned[targets:], x_v[right, :], preferred_element_type=f32)
                    if place:
                        grad += gacc[...]
                    gacc[...] = grad
                slot = step % 2
                exchange = pltpu.make_async_remote_copy(
                    src_ref=gacc, dst_ref=gx.at[slot], send_sem=gx_send, recv_sem=gx_recv.at[slot],
                    device_id=sibling, device_id_type=MESH_ID)
                exchange.start()
                wait_rows(rs, half - chunk, rs_send)
                wait_rows(rs, half - chunk, ag_send)
                exchange.wait_recv()
                gradient = (gacc[...] + gx[slot]) * (1.0 / samples)
                delta = eta_ref[...] * (gradient - ridge * wt[...])
                wt[...] = wt[...] + COMBINE_WEIGHT * delta
                empty = jnp.zeros((targets, 128), f32)
                for col in range(feat_len // 128):
                    span = slice(col * 128, (col + 1) * 128)
                    wl[span, :] = jnp.transpose(jnp.concatenate([delta[:, span], empty], axis=0)).astype(bf16)
                    wr[span, :] = jnp.transpose(jnp.concatenate([empty, delta[:, span]], axis=0)).astype(bf16)
                exchange.wait_send()
                return 0

            lax.fori_loop(0, SWEEPS, sweep, 0)
            wt_copy = pltpu.make_async_copy(wt, wt_out, in_sem.at[0])
            wt_copy.start()
            send_terms(lambda order: None)
            reduce_terms(COMBINE_WEIGHT)
            rf[rows_of(me), :] = rown[...]
            send_owned(rf.at[rows_of(me)], rf)
            out_copies = []
            for dz in NEAR_FIRST:
                wait_rows(rf, group(dz), ag_recv.at[dz])
                block = pl.ds(pl.multiple_of(from_plane(dz) * plane, plane), plane)
                out_copies.append(pltpu.make_async_copy(rf.at[block], rp_out.at[block], out_sem.at[dz]))
                out_copies[-1].start()
            wait_rows(rs, half - chunk, rs_send)
            wait_rows(rf, half - chunk, ag_send)
            wt_copy.wait()
            for copy in out_copies:
                copy.wait()

        any_space = pl.BlockSpec(memory_space=pl.ANY)
        vmem = pl.BlockSpec(memory_space=pltpu.VMEM)
        return pl.pallas_call(
            kernel,
            name="ridge_sweeps",
            out_shape=(jax.ShapeDtypeStruct((targets, feat_len), f32), jax.ShapeDtypeStruct((half, lanes), f32)),
            in_specs=[any_space, any_space, any_space, vmem],
            out_specs=(any_space, any_space),
            scratch_shapes=[
                pltpu.VMEM((rows, feat_len), bf16),
                pltpu.VMEM((feat_len, targets), f32),
                pltpu.VMEM((2, chunk, targets), f32),
                pltpu.VMEM((half, lanes), bf16),
                pltpu.VMEM((half, lanes), bf16),
                pltpu.VMEM((half, lanes), bf16),
                pltpu.VMEM((chunk, lanes), f32),
                pltpu.VMEM((half, lanes), f32),
                pltpu.VMEM((targets, feat_len), f32),
                pltpu.VMEM((targets, feat_len), f32),
                pltpu.VMEM((2, targets, feat_len), f32),
                pltpu.VMEM((feat_len, lanes), bf16),
                pltpu.VMEM((feat_len, lanes), bf16),
                pltpu.SemaphoreType.DMA((2 * SIDE,)),
                pltpu.SemaphoreType.DMA((3,)),
                pltpu.SemaphoreType.DMA,
                pltpu.SemaphoreType.DMA((SIDE,)),
                pltpu.SemaphoreType.DMA,
                pltpu.SemaphoreType.DMA((SIDE,)),
                pltpu.SemaphoreType.DMA,
                pltpu.SemaphoreType.DMA((2,)),
                pltpu.SemaphoreType.DMA((SIDE,)),
            ],
            compiler_params=pltpu.CompilerParams(collective_id=0, has_side_effects=True),
        )

    def local_solve(x_loc, w_loc, y_loc, eta_loc):
        rows_loc, feat_len = x_loc.shape
        targets = w_loc.shape[1]
        samples = rows_loc * samp_count
        ridge = RIDGE_SCALE * (feat_len * feat_count) / samples
        call = make_kernel(rows_loc, feat_len, targets, ridge, samples)
        weights_turned, packed = call(x_loc, w_loc, y_loc, eta_loc.reshape(1, feat_len))
        residual = jnp.concatenate([packed[:, :targets], packed[:, targets:]], axis=0)
        return weights_turned.T, residual

    return jax.shard_map(
        local_solve,
        mesh=mesh,
        in_specs=(P(("prob", "samp"), "feat"), P(("prob", "feat"), None), P(("prob", "samp"), None), P(("prob", "feat"))),
        out_specs=(P(("prob", "feat"), None), P(("prob", "samp"), None)),
        check_vma=False,
    )
```

time: 829 us -> 141 us (0.17)
  waiting for transfers between devices: 748 us -> 0 us
  Pallas kernels: 0 us -> 130 us
  matrix products: 59 us -> 0 us
  between operations: 13.9 us -> 0.66 us
  local copies, waits for them, and re-layouts: 0.04 us -> 9.31 us
    psum x9 -> x0, waiting for transfers between devices: 748 us -> none  [the longest x4 522 us: local_solve(): lax.psum(update.astype(jnp.bfloat16).astype(jnp.float32), 'feat')]
    pallas_call x0 -> x1, Pallas kernels: none -> 130 us  [local_solve(): call(x_loc, w_loc, y_loc, eta_loc.reshape(1, feat_len))]
    dot_general x9 -> x0, matrix products: 59 us -> none  [the longest x4 28.5 us: local_solve(): jnp.dot(x_loc, delta.astype(jnp.bfloat16), preferred_element_type=jnp.flo...]
  transfers between devices with their start and end apart: 9 -> 0, of which waited for: 9 -> 0; matrix products, arithmetic and copies ran while one was open for 0% -> 0% of each run, Pallas kernels for 0% -> 0%
where the time goes in v1:
time: 141 us; the launch traced here: 140 us
  Pallas kernels  130 us (92%)
  local copies, waits for them, and re-layouts  9.31 us (7%)
    pallas_call x1, Pallas kernels, local_solve(): call(x_loc, w_loc, y_loc, eta_loc.reshape(1, feat_len))  130 us
    unnamed x6, local copies, waits for them, and re-layouts  7.39 us

profile of v1, /device:TPU:1, one launch (start us, length us, event | category | flops | bytes accessed | tf_op | source)
XLA Modules:
  0.0 140.2 jit_solution(15268266035875884708)
XLA Ops:
  0.6 1.9 %copy.6.w_hbm = f32[1024,64]{1,0:T(8,128)} copy(f32[1024,64]{0,1:T(8,128)} %param.5) | data formatting | bytes 524288 | tf_op args[1]
  2.6 3.2 %copy.7.y_hbm = f32[4096,64]{1,0:T(8,128)} copy(f32[4096,64]{0,1:T(8,128)} %param.6) | data formatting | bytes 2097152 | tf_op args[2]
  5.7 130.1 %ridge_sweeps.1 = (f32[64,1024]{1,0:T(8,128)}, f32[2048,128]{1,0:T(8,128)}) custom-call(bf16[4096,1024]{1,0:T(8,128)(2,1)} %x_hbm.1, f32[1024,64]{1,0:T(8,128)} %copy.6.w_hbm, f32[4096,64]{1,0:T(8,128)} %copy.7.y_hbm, f32[1,1024]{1,0:T(1,128)} %bitcast.3), custom_call_target="tpu_custom_call" | custom-call | tf_op jit(solution)/shard_map/ridge_sweeps/pallas_call | solution.py:231
  135.9 1.9 %fusion = (f32[2048,64]{1,0:T(8,128)S(1)}, f32[2048,64]{1,0:T(8,128)S(1)}) fusion(f32[2048,128]{1,0:T(8,128)} %get-tuple-element.5), kind=kLoop, calls=%fused_computation.1 | loop fusion | bytes 2097152 | tf_op jit(solution)/shard_map/slice | solution.py:232
  137.8 0.1 pad_maximum_fusion
  138.0 0.0 copy-start
  138.0 1.6 %copy.8 = f32[4096,64]{0,1:T(8,128)} copy(f32[4096,64]{1,0:T(8,128)S(1)} %pad_maximum_fusion) | data formatting | bytes 2097152
  139.5 0.0 copy-done
  139.5 0.7 copy.10
Async XLA Ops:
  138.0 1.6 %copy-start = (f32[64,1024]{1,0:T(8,128)S(1)}, f32[64,1024]{1,0:T(8,128)}, u32[]{:S(2)}) copy-start(f32[64,1024]{1,0:T(8,128)} %get-tuple-element.4) | copy-start | bytes 786436

commit v2 on v0

v2 whole, which is shorter than its diff:
```python
import jax
import jax.numpy as jnp
from jax import lax
from jax.experimental import pallas as pl
from jax.experimental.pallas import tpu as pltpu
from jax.sharding import PartitionSpec as P

SWEEPS = 4
COMBINE_WEIGHT = 0.8
RIDGE_SCALE = 0.1
SIDE = 4
MESH_ID = pl.DeviceIdType.MESH

PLANE = sorted(
    [(dx, dy) for dy in range(SIDE) for dx in range(SIDE)],
    key=lambda d: -(min(d[0], SIDE - d[0]) + min(d[1], SIDE - d[1])),
)
FAR_FIRST = (2, 1, 3, 0)
NEAR_FIRST = (0, 1, 3, 2)
TURNED = (((1,), (1,)), ((), ()))


def solution(mesh):
    samp_count = mesh.shape["samp"]
    feat_count = mesh.shape["feat"]
    assert feat_count == SIDE**3 and samp_count == 2

    def make_kernel(rows, feat_len, targets, ridge, samples):
        plane = rows // SIDE
        tall = targets // SIDE
        wide = plane // SIDE
        f32, bf16 = jnp.float32, jnp.bfloat16

        def kernel(x_hbm, w_hbm, y_hbm, eta_ref, w_out, r_out, x_v, xt, ub, rs, rb, rown, wt, wb, gacc, gx,
                   x_sem, in_sem, rs_send, rs_recv, ag_send, ag_recv, gx_send, gx_recv):
            samp = lax.axis_index("samp")
            me = lax.axis_index("feat")
            cx, cy, cz = me % SIDE, (me // SIDE) % SIDE, me // (SIDE * SIDE)
            nx = [(cx + d) % SIDE for d in range(SIDE)]
            ny = [(cy + d) % SIDE for d in range(SIDE)]
            nz = [(cz + d) % SIDE for d in range(SIDE)]
            sibling = (0, 1 - samp, me)

            def peer_of(dx, dy, dz):
                return (0, samp, nz[dz] * (SIDE * SIDE) + ny[dy] * SIDE + nx[dx])

            def others(dz):
                return [(dx, dy) for dx, dy in PLANE if (dx, dy, dz) != (0, 0, 0)]

            def tall_at(x):
                return pl.ds(pl.multiple_of(x * tall, tall), tall)

            def wide_at(y):
                return pl.ds(pl.multiple_of(y * wide, wide), wide)

            def plane_at(z):
                return pl.ds(pl.multiple_of(z * plane, plane), plane)

            own_samples = pl.ds(pl.multiple_of(cz * plane + cy * wide, wide), wide)

            w_copy = pltpu.make_async_copy(w_hbm, wt, in_sem.at[0])
            w_copy.start()
            x_copies = []
            for order, dz in enumerate(FAR_FIRST):
                x_copies.append(pltpu.make_async_copy(x_hbm.at[plane_at(nz[dz])], x_v.at[plane_at(nz[dz])], x_sem.at[order]))
                x_copies[-1].start()
            y_copy = pltpu.make_async_copy(y_hbm.at[tall_at(cx), own_samples], rown, in_sem.at[1])
            y_copy.start()

            barrier = pltpu.get_barrier_semaphore()
            pl.semaphore_signal(barrier, inc=1, device_id=sibling, device_id_type=MESH_ID)
            for dz in FAR_FIRST:
                for dx, dy in others(dz):
                    pl.semaphore_signal(barrier, inc=1, device_id=peer_of(dx, dy, dz), device_id_type=MESH_ID)

            w_copy.wait()
            wb[...] = wt[...].astype(bf16)
            y_copy.wait()

            def send_terms(term_of):
                for order, dz in enumerate(FAR_FIRST):
                    term_of(order, nz[dz])
                    for dx, dy in others(dz):
                        pltpu.make_async_remote_copy(
                            src_ref=ub.at[nz[dz], tall_at(nx[dx]), wide_at(ny[dy])], dst_ref=rs.at[me], send_sem=rs_send,
                            recv_sem=rs_recv.at[dz], device_id=peer_of(dx, dy, dz), device_id_type=MESH_ID).start()
                rs[me] = ub[cz, tall_at(cx), wide_at(cy)]

            def later_term(order, z):
                ub[z] = jnp.dot(wb[...], xt[z], preferred_element_type=f32).astype(bf16)

            def wait_bytes(ref, sem):
                pltpu.make_async_copy(ref, ref, sem).wait()

            per_plane = SIDE * SIDE

            def group(dz):
                return per_plane - 1 if dz == 0 else per_plane

            def reduce_terms(scale):
                for dz in NEAR_FIRST:
                    wait_bytes(rs.at[pl.ds(0, group(dz))], rs_recv.at[dz])
                total = rs[0].astype(f32)
                for index in range(1, feat_count):
                    total += rs[index].astype(f32)
                rown[...] = rown[...] - scale * total

            def from_plane(dz):
                return nz[(SIDE - dz) % SIDE]

            def sweep(step, unused):
                def term_of(order, z):
                    @pl.when(step == 0)
                    def _():
                        x_copies[order].wait()
                        ub[z] = lax.dot_general(wb[...], x_v[plane_at(z), :], TURNED, preferred_element_type=f32).astype(bf16)
                        if order == 0:
                            pl.semaphore_wait(barrier, feat_count)

                    @pl.when(step > 0)
                    def _():
                        later_term(order, z)

                send_terms(term_of)

                @pl.when(step == 0)
                def _():
                    def turn(index, unused):
                        z, col = index // (feat_len // 128), index % (feat_len // 128)
                        lanes = pl.ds(pl.multiple_of(col * 128, 128), 128)
                        xt[z, lanes, :] = jnp.transpose(x_v[plane_at(z), lanes])
                        return 0

                    lax.fori_loop(0, SIDE * (feat_len // 128), turn, 0)

                reduce_terms(jnp.where(step == 0, 1.0, COMBINE_WEIGHT))
                mine = rb.at[cz, tall_at(cx), wide_at(cy)]
                mine[...] = rown[...].astype(bf16)
                for dz in FAR_FIRST:
                    for dx, dy in others(dz):
                        pltpu.make_async_remote_copy(
                            src_ref=mine, dst_ref=mine, send_sem=ag_send, recv_sem=ag_recv.at[dz],
                            device_id=peer_of(dx, dy, dz), device_id_type=MESH_ID).start()
                for place, dz in enumerate(NEAR_FIRST):
                    wait_bytes(rs.at[pl.ds(0, group(dz))], ag_recv.at[dz])
                    source = from_plane(dz)
                    grad = jnp.dot(rb[source], x_v[plane_at(source), :], preferred_element_type=f32)
                    if place:
                        grad += gacc[...]
                    gacc[...] = grad
                slot = step % 2
                exchange = pltpu.make_async_remote_copy(
                    src_ref=gacc, dst_ref=gx.at[slot], send_sem=gx_send, recv_sem=gx_recv.at[slot],
                    device_id=sibling, device_id_type=MESH_ID)
                exchange.start()
                wait_bytes(rs.at[pl.ds(0, feat_count - 1)], rs_send)
                wait_bytes(rs.at[pl.ds(0, feat_count - 1)], ag_send)
                exchange.wait_recv()
                gradient = (gacc[...] + gx[slot]) * (1.0 / samples)
                delta = eta_ref[...] * (gradient - ridge * wt[...])
                wt[...] = wt[...] + COMBINE_WEIGHT * delta
                wb[...] = delta.astype(bf16)
                exchange.wait_send()
                return 0

            lax.fori_loop(0, SWEEPS, sweep, 0)
            w_copy = pltpu.make_async_copy(wt, w_out, in_sem.at[0])
            w_copy.start()
            send_terms(later_term)
            reduce_terms(COMBINE_WEIGHT)
            mine = r_out.at[tall_at(cx), own_samples]
            y_copy = pltpu.make_async_copy(rown, mine, in_sem.at[1])
            y_copy.start()
            for dz in FAR_FIRST:
                for dx, dy in others(dz):
                    pltpu.make_async_remote_copy(
                        src_ref=rown, dst_ref=mine, send_sem=ag_send, recv_sem=ag_recv.at[dz],
                        device_id=peer_of(dx, dy, dz), device_id_type=MESH_ID).start()
            w_copy.wait()
            y_copy.wait()
            wait_bytes(rs.at[pl.ds(0, feat_count - 1)], rs_send)
            ratio = 2
            for dz in NEAR_FIRST:
                wait_bytes(rs.at[pl.ds(0, ratio * group(dz))], ag_recv.at[dz])
            sent = ratio * (feat_count - 1) * tall * wide // plane
            wait_bytes(xt.at[0, pl.ds(0, sent)], ag_send)

        any_space = pl.BlockSpec(memory_space=pl.ANY)
        vmem = pl.BlockSpec(memory_space=pltpu.VMEM)
        return pl.pallas_call(
            kernel,
            name="ridge_sweeps",
            out_shape=(jax.ShapeDtypeStruct((targets, feat_len), f32), jax.ShapeDtypeStruct((targets, rows), f32)),
            in_specs=[any_space, any_space, any_space, vmem],
            out_specs=(any_space, any_space),
            scratch_shapes=[
                pltpu.VMEM((rows, feat_len), bf16),
                pltpu.VMEM((SIDE, feat_len, plane), bf16),
                pltpu.VMEM((SIDE, targets, plane), bf16),
                pltpu.VMEM((feat_count, tall, wide), bf16),
                pltpu.VMEM((SIDE, targets, plane), bf16),
                pltpu.VMEM((tall, wide), f32),
                pltpu.VMEM((targets, feat_len), f32),
                pltpu.VMEM((targets, feat_len), bf16),
                pltpu.VMEM((targets, feat_len), f32),
                pltpu.VMEM((2, targets, feat_len), f32),
                pltpu.SemaphoreType.DMA((SIDE,)),
                pltpu.SemaphoreType.DMA((2,)),
                pltpu.SemaphoreType.DMA,
                pltpu.SemaphoreType.DMA((SIDE,)),
                pltpu.SemaphoreType.DMA,
                pltpu.SemaphoreType.DMA((SIDE,)),
                pltpu.SemaphoreType.DMA,
                pltpu.SemaphoreType.DMA((2,)),
            ],
            compiler_params=pltpu.CompilerParams(collective_id=0, has_side_effects=True),
        )

    def local_solve(x_loc, w_loc, y_loc, eta_loc):
        rows_loc, feat_len = x_loc.shape
        targets = w_loc.shape[1]
        samples = rows_loc * samp_count
        ridge = RIDGE_SCALE * (feat_len * feat_count) / samples
        call = make_kernel(rows_loc, feat_len, targets, ridge, samples)
        weights, residual = call(x_loc, w_loc.T, y_loc.T, eta_loc.reshape(1, feat_len))
        return weights.T, residual.T

    return jax.shard_map(
        local_solve,
        mesh=mesh,
        in_specs=(P(("prob", "samp"), "feat"), P(("prob", "feat"), None), P(("prob", "samp"), None), P(("prob", "feat"))),
        out_specs=(P(("prob", "feat"), None), P(("prob", "samp"), None)),
        check_vma=False,
    )
```

time: 829 us -> 127 us (0.15)
  waiting for transfers between devices: 748 us -> 0 us
  Pallas kernels: 0 us -> 122 us
  matrix products: 59 us -> 0 us
  between operations: 13.9 us -> 0.64 us
    psum x9 -> x0, waiting for transfers between devices: 748 us -> none  [the longest x4 522 us: local_solve(): lax.psum(update.astype(jnp.bfloat16).astype(jnp.float32), 'feat')]
    pallas_call x0 -> x1, Pallas kernels: none -> 122 us  [local_solve(): call(x_loc, w_loc.T, y_loc.T, eta_loc.reshape(1, feat_len))]
    dot_general x9 -> x0, matrix products: 59 us -> none  [the longest x4 28.5 us: local_solve(): jnp.dot(x_loc, delta.astype(jnp.bfloat16), preferred_element_type=jnp.flo...]
  transfers between devices with their start and end apart: 9 -> 0, of which waited for: 9 -> 0; matrix products, arithmetic and copies ran while one was open for 0% -> 0% of each run, Pallas kernels for 0% -> 0%
where the time goes in v2:
time: 127 us; the launch traced here: 126 us
  Pallas kernels  122 us (96%)
  local copies, waits for them, and re-layouts  3.94 us (3%)
    pallas_call x1, Pallas kernels, local_solve(): call(x_loc, w_loc.T, y_loc.T, eta_loc.reshape(1, feat_len))  122 us
    unnamed x2, local copies, waits for them, and re-layouts  3.94 us

profile of v2, /device:TPU:1, one launch (start us, length us, event | category | flops | bytes accessed | tf_op | source)
XLA Modules:
  0.0 126.3 jit_solution(15515300953750537424)
XLA Ops:
  0.6 121.7 %ridge_sweeps.1 = (f32[64,1024]{1,0:T(8,128)}, f32[64,4096]{1,0:T(8,128)}) custom-call(bf16[4096,1024]{1,0:T(8,128)(2,1)} %x_hbm.1, f32[64,1024]{1,0:T(8,128)} %bitcast.7, f32[64,4096]{1,0:T(8,128)} %bitcast.5, f32[1,1024]{1,0:T(1,128)} %bitcast.9), custom_call_target="tpu_custom_call" | custom-call | tf_op jit(solution)/shard_map/ridge_sweeps/pallas_call | solution.py:225
  122.4 1.7 %copy.8 = f32[1024,64]{0,1:T(8,128)} copy(f32[1024,64]{0,1:T(8,128)} %bitcast.8) | data formatting | bytes 524288
  124.0 2.3 %copy.9 = f32[4096,64]{0,1:T(8,128)} copy(f32[4096,64]{0,1:T(8,128)} %bitcast.6) | data formatting | bytes 2097152

commit v3 on v0

v3 whole, which is shorter than its diff:
```python
import jax
import jax.numpy as jnp
from jax import lax
from jax.experimental import pallas as pl
from jax.experimental.pallas import tpu as pltpu
from jax.sharding import PartitionSpec as P

SWEEPS = 4
COMBINE_WEIGHT = 0.8
RIDGE_SCALE = 0.1
SIDE = 4
GROUPS = 2
MESH_ID = pl.DeviceIdType.MESH

PLANE = sorted(
    [(dx, dy) for dy in range(SIDE) for dx in range(SIDE)],
    key=lambda d: -(min(d[0], SIDE - d[0]) + min(d[1], SIDE - d[1])),
)
FAR_FIRST = (2, 1, 3, 0)
TURNED = (((1,), (1,)), ((), ()))


def solution(mesh):
    samp_count = mesh.shape["samp"]
    feat_count = mesh.shape["feat"]
    assert feat_count == SIDE**3 and samp_count == 2

    def make_kernel(rows, feat_len, targets, ridge, samples):
        f32, bf16 = jnp.float32, jnp.bfloat16
        plane = rows // SIDE
        height = targets // GROUPS
        tall = 16
        stacks = height // tall
        wide = plane * stacks // (SIDE * SIDE)
        per_plane = SIDE * SIDE

        def kernel(x_hbm, w_hbm, y_hbm, eta_ref, w_out, r_out, x_v, xt, ub, rs, rb, rown, wt, wb, gacc, gx,
                   x_sem, in_sem, y_sem, rs_send, rs_recv, ag_send, ag_recv, gx_send, gx_recv):
            samp = lax.axis_index("samp")
            me = lax.axis_index("feat")
            cx, cy, cz = me % SIDE, (me // SIDE) % SIDE, me // (SIDE * SIDE)
            nx = [(cx + d) % SIDE for d in range(SIDE)]
            ny = [(cy + d) % SIDE for d in range(SIDE)]
            nz = [(cz + d) % SIDE for d in range(SIDE)]
            sibling = (0, 1 - samp, me)
            tall_of = [pl.multiple_of((x % stacks) * tall, tall) for x in nx]
            wide_of = [x // stacks * wide for x in nx]
            lane_of = [y * (SIDE // stacks) * wide for y in ny]

            def peer_of(dx, dy, dz):
                return (0, samp, nz[dz] * per_plane + ny[dy] * SIDE + nx[dx])

            def others(dz):
                return [(dx, dy) for dx, dy in PLANE if (dx, dy, dz) != (0, 0, 0)]

            def chunk_of(dx, dy):
                return pl.ds(tall_of[dx], tall), pl.ds(pl.multiple_of(lane_of[dy] + wide_of[dx], wide), wide)

            def plane_at(z):
                return pl.ds(pl.multiple_of(z * plane, plane), plane)

            def output_at(group):
                lane = pl.multiple_of(cz * plane + lane_of[0] + wide_of[0], wide)
                return pl.ds(pl.multiple_of(group * height + tall_of[0], tall), tall), pl.ds(lane, wide)

            def group_rows(group):
                return slice(group * height, (group + 1) * height)

            def wait_bytes(ref, sem):
                pltpu.make_async_copy(ref, ref, sem).wait()

            def count(dz):
                return per_plane - 1 if dz == 0 else per_plane

            w_copy = pltpu.make_async_copy(w_hbm, wt, in_sem)
            w_copy.start()
            x_copies = []
            for order, dz in enumerate(FAR_FIRST):
                x_copies.append(pltpu.make_async_copy(x_hbm.at[plane_at(nz[dz])], x_v.at[plane_at(nz[dz])], x_sem.at[order]))
                x_copies[-1].start()
            y_copies = []
            for group in range(GROUPS):
                y_copies.append(pltpu.make_async_copy(y_hbm.at[output_at(group)], rown.at[group], y_sem.at[group]))
                y_copies[-1].start()

            barrier = pltpu.get_barrier_semaphore()
            pl.semaphore_signal(barrier, inc=1, device_id=sibling, device_id_type=MESH_ID)
            for dz in FAR_FIRST:
                for dx, dy in others(dz):
                    pl.semaphore_signal(barrier, inc=1, device_id=peer_of(dx, dy, dz), device_id_type=MESH_ID)

            def send_plane(group, dz):
                for dx, dy in others(dz):
                    pltpu.make_async_remote_copy(
                        src_ref=ub.at[(group, nz[dz], *chunk_of(dx, dy))], dst_ref=rs.at[group * feat_count + me], send_sem=rs_send.at[group],
                        recv_sem=rs_recv.at[group, dz], device_id=peer_of(dx, dy, dz), device_id_type=MESH_ID).start()

            def keep_own(group):
                rs[group * feat_count + me] = ub[(group, cz, *chunk_of(0, 0))]

            def send_terms(group):
                for dz in FAR_FIRST:
                    ub[group, nz[dz]] = jnp.dot(wb[group_rows(group), :], xt[nz[dz]], preferred_element_type=f32).astype(bf16)
                    send_plane(group, dz)
                keep_own(group)

            def reduce_terms(group, scale):
                for dz in FAR_FIRST:
                    wait_bytes(rs.at[pl.ds(0, count(dz))], rs_recv.at[group, dz])
                total = rs[group * feat_count].astype(f32)
                for index in range(1, feat_count):
                    total += rs[group * feat_count + index].astype(f32)
                rown[group] = rown[group] - scale * total

            def send_owned(group, src, dst):
                for dz in FAR_FIRST:
                    for dx, dy in others(dz):
                        pltpu.make_async_remote_copy(
                            src_ref=src, dst_ref=dst, send_sem=ag_send.at[group], recv_sem=ag_recv.at[group, dz],
                            device_id=peer_of(dx, dy, dz), device_id_type=MESH_ID).start()

            def share_residual(group):
                mine = rb.at[(group, cz, *chunk_of(0, 0))]
                mine[...] = rown[group].astype(bf16)
                send_owned(group, mine, mine)

            def step_weights(group, slot):
                for place, dz in enumerate(FAR_FIRST):
                    wait_bytes(rs.at[pl.ds(0, count(dz))], ag_recv.at[group, dz])
                    source = nz[(SIDE - dz) % SIDE]
                    grad = jnp.dot(rb[group, source], x_v[plane_at(source), :], preferred_element_type=f32)
                    if place:
                        grad += gacc[group]
                    gacc[group] = grad
                exchange = pltpu.make_async_remote_copy(
                    src_ref=gacc.at[group], dst_ref=gx.at[group, slot], send_sem=gx_send.at[group],
                    recv_sem=gx_recv.at[group, slot], device_id=sibling, device_id_type=MESH_ID)
                exchange.start()
                sent = rs.at[pl.ds(0, feat_count - 1)]
                wait_bytes(sent, rs_send.at[group])
                wait_bytes(sent, ag_send.at[group])
                exchange.wait_recv()
                part = group_rows(group)
                gradient = (gacc[group] + gx[group, slot]) * (1.0 / samples)
                delta = eta_ref[...] * (gradient - ridge * wt[part, :])
                wt[part, :] = wt[part, :] + COMBINE_WEIGHT * delta
                wb[part, :] = delta.astype(bf16)
                exchange.wait_send()

            w_copy.wait()
            wb[...] = wt[...].astype(bf16)
            for order, dz in enumerate(FAR_FIRST):
                x_copies[order].wait()
                first = lax.dot_general(wb[...], x_v[plane_at(nz[dz]), :], TURNED, preferred_element_type=f32)
                for group in range(GROUPS):
                    ub[group, nz[dz]] = first[group_rows(group), :].astype(bf16)
                if order == 0:
                    pl.semaphore_wait(barrier, feat_count)
                for group in range(GROUPS):
                    send_plane(group, dz)
            for group in range(GROUPS):
                keep_own(group)
                y_copies[group].wait()

            def turn(index, unused):
                z, col = index // (feat_len // 128), index % (feat_len // 128)
                lanes = pl.ds(pl.multiple_of(col * 128, 128), 128)
                xt[z, lanes, :] = jnp.transpose(x_v[plane_at(z), lanes])
                return 0

            lax.fori_loop(0, SIDE * (feat_len // 128), turn, 0)

            def sweep(step, unused):
                scale = jnp.where(step == 0, 1.0, COMBINE_WEIGHT)
                for group in range(GROUPS):
                    reduce_terms(group, scale)
                    share_residual(group)
                for group in range(GROUPS):
                    step_weights(group, step % 2)
                    send_terms(group)
                return 0

            lax.fori_loop(0, SWEEPS, sweep, 0)
            w_copy = pltpu.make_async_copy(wt, w_out, in_sem)
            w_copy.start()
            y_copies = []
            for group in range(GROUPS):
                reduce_terms(group, COMBINE_WEIGHT)
                mine = r_out.at[output_at(group)]
                y_copies.append(pltpu.make_async_copy(rown.at[group], mine, y_sem.at[group]))
                y_copies[-1].start()
                send_owned(group, rown.at[group], mine)
            w_copy.wait()
            ratio = 2
            for group in range(GROUPS):
                y_copies[group].wait()
                wait_bytes(rs.at[pl.ds(0, feat_count - 1)], rs_send.at[group])
                for dz in FAR_FIRST:
                    wait_bytes(rs.at[pl.ds(0, ratio * count(dz))], ag_recv.at[group, dz])
                wait_bytes(rs.at[pl.ds(0, ratio * (feat_count - 1))], ag_send.at[group])

        any_space = pl.BlockSpec(memory_space=pl.ANY)
        vmem = pl.BlockSpec(memory_space=pltpu.VMEM)
        return pl.pallas_call(
            kernel,
            name="ridge_sweeps",
            out_shape=(jax.ShapeDtypeStruct((targets, feat_len), f32), jax.ShapeDtypeStruct((targets, rows), f32)),
            in_specs=[any_space, any_space, any_space, vmem],
            out_specs=(any_space, any_space),
            scratch_shapes=[
                pltpu.VMEM((rows, feat_len), bf16),
                pltpu.VMEM((SIDE, feat_len, plane), bf16),
                pltpu.VMEM((GROUPS, SIDE, height, plane), bf16),
                pltpu.VMEM((GROUPS * feat_count, tall, wide), bf16),
                pltpu.VMEM((GROUPS, SIDE, height, plane), bf16),
                pltpu.VMEM((GROUPS, tall, wide), f32),
                pltpu.VMEM((targets, feat_len), f32),
                pltpu.VMEM((targets, feat_len), bf16),
                pltpu.VMEM((GROUPS, height, feat_len), f32),
                pltpu.VMEM((GROUPS, 2, height, feat_len), f32),
                pltpu.SemaphoreType.DMA((SIDE,)),
                pltpu.SemaphoreType.DMA,
                pltpu.SemaphoreType.DMA((GROUPS,)),
                pltpu.SemaphoreType.DMA((GROUPS,)),
                pltpu.SemaphoreType.DMA((GROUPS, SIDE)),
                pltpu.SemaphoreType.DMA((GROUPS,)),
                pltpu.SemaphoreType.DMA((GROUPS, SIDE)),
                pltpu.SemaphoreType.DMA((GROUPS,)),
                pltpu.SemaphoreType.DMA((GROUPS, 2)),
            ],
            compiler_params=pltpu.CompilerParams(collective_id=0, has_side_effects=True),
        )

    def local_solve(x_loc, w_loc, y_loc, eta_loc):
        rows_loc, feat_len = x_loc.shape
        targets = w_loc.shape[1]
        samples = rows_loc * samp_count
        ridge = RIDGE_SCALE * (feat_len * feat_count) / samples
        call = make_kernel(rows_loc, feat_len, targets, ridge, samples)
        weights, residual = call(x_loc, w_loc.T, y_loc.T, eta_loc.reshape(1, feat_len))
        return weights.T, residual.T

    return jax.shard_map(
        local_solve,
        mesh=mesh,
        in_specs=(P(("prob", "samp"), "feat"), P(("prob", "feat"), None), P(("prob", "samp"), None), P(("prob", "feat"))),
        out_specs=(P(("prob", "feat"), None), P(("prob", "samp"), None)),
        check_vma=False,
    )
```

time: 829 us -> 108 us (0.13)
  waiting for transfers between devices: 748 us -> 0 us
  Pallas kernels: 0 us -> 103 us
  matrix products: 59 us -> 0 us
  between operations: 13.9 us -> 0.64 us
    psum x9 -> x0, waiting for transfers between devices: 748 us -> none  [the longest x4 522 us: local_solve(): lax.psum(update.astype(jnp.bfloat16).astype(jnp.float32), 'feat')]
    pallas_call x0 -> x1, Pallas kernels: none -> 103 us  [local_solve(): call(x_loc, w_loc.T, y_loc.T, eta_loc.reshape(1, feat_len))]
    dot_general x9 -> x0, matrix products: 59 us -> none  [the longest x4 28.5 us: local_solve(): jnp.dot(x_loc, delta.astype(jnp.bfloat16), preferred_element_type=jnp.flo...]
  transfers between devices with their start and end apart: 9 -> 0, of which waited for: 9 -> 0; matrix products, arithmetic and copies ran while one was open for 0% -> 0% of each run, Pallas kernels for 0% -> 0%
where the time goes in v3:
time: 108 us; the launch traced here: 107 us
  Pallas kernels  103 us (95%)
  local copies, waits for them, and re-layouts  3.94 us (4%)
    pallas_call x1, Pallas kernels, local_solve(): call(x_loc, w_loc.T, y_loc.T, eta_loc.reshape(1, feat_len))  103 us
    unnamed x2, local copies, waits for them, and re-layouts  3.94 us

profile of v3, /device:TPU:1, one launch (start us, length us, event | category | flops | bytes accessed | tf_op | source)
XLA Modules:
  0.0 107.5 jit_solution(9713004741254316604)
XLA Ops:
  0.6 102.9 %ridge_sweeps.1 = (f32[64,1024]{1,0:T(8,128)}, f32[64,4096]{1,0:T(8,128)}) custom-call(bf16[4096,1024]{1,0:T(8,128)(2,1)} %x_hbm.1, f32[64,1024]{1,0:T(8,128)} %bitcast.7, f32[64,4096]{1,0:T(8,128)} %bitcast.5, f32[1,1024]{1,0:T(1,128)} %bitcast.9), custom_call_target="tpu_custom_call" | custom-call | tf_op jit(solution)/shard_map/ridge_sweeps/pallas_call | solution.py:240
  103.5 1.7 %copy.8 = f32[1024,64]{0,1:T(8,128)} copy(f32[1024,64]{0,1:T(8,128)} %bitcast.8) | data formatting | bytes 524288
  105.2 2.3 %copy.9 = f32[4096,64]{0,1:T(8,128)} copy(f32[4096,64]{0,1:T(8,128)} %bitcast.6) | data formatting | bytes 2097152

commit v4 on v3

--- a/solution.py
+++ b/solution.py
@@ -156,8 +156,9 @@
                     ub[group, nz[dz]] = first[group_rows(group), :].astype(bf16)
                 if order == 0:
                     pl.semaphore_wait(barrier, feat_count)
-                for group in range(GROUPS):
-                    send_plane(group, dz)
+                send_plane(0, dz)
+            for dz in FAR_FIRST:
+                send_plane(1, dz)
             for group in range(GROUPS):
                 keep_own(group)
                 y_copies[group].wait()

time: 108 us -> 106 us (0.981)
    pallas_call x1, Pallas kernels: 103 us -> 102 us  [local_solve(): call(x_loc, w_loc.T, y_loc.T, eta_loc.reshape(1, feat_len))]
where the time goes in v4:
time: 106 us
  Pallas kernels  102 us (96%)
  local copies, waits for them, and re-layouts  3.94 us (4%)
    pallas_call x1, Pallas kernels, local_solve(): call(x_loc, w_loc.T, y_loc.T, eta_loc.reshape(1, feat_len))  102 us
    unnamed x2, local copies, waits for them, and re-layouts  3.94 us

profile of v4, /device:TPU:1, one launch (start us, length us, event | category | flops | bytes accessed | tf_op | source)
XLA Modules:
  0.0 106.2 jit_solution(12849330191361103953)
XLA Ops:
  0.6 101.6 %ridge_sweeps.1 = (f32[64,1024]{1,0:T(8,128)}, f32[64,4096]{1,0:T(8,128)}) custom-call(bf16[4096,1024]{1,0:T(8,128)(2,1)} %x_hbm.1, f32[64,1024]{1,0:T(8,128)} %bitcast.7, f32[64,4096]{1,0:T(8,128)} %bitcast.5, f32[1,1024]{1,0:T(1,128)} %bitcast.9), custom_call_target="tpu_custom_call" | custom-call | tf_op jit(solution)/shard_map/ridge_sweeps/pallas_call | solution.py:241
  102.3 1.7 %copy.8 = f32[1024,64]{0,1:T(8,128)} copy(f32[1024,64]{0,1:T(8,128)} %bitcast.8) | data formatting | bytes 524288
  103.9 2.3 %copy.9 = f32[4096,64]{0,1:T(8,128)} copy(f32[4096,64]{0,1:T(8,128)} %bitcast.6) | data formatting | bytes 2097152

commit v5 on v4

--- a/solution.py
+++ b/solution.py
@@ -34,8 +34,10 @@
         wide = plane * stacks // (SIDE * SIDE)
         per_plane = SIDE * SIDE
 
-        def kernel(x_hbm, w_hbm, y_hbm, eta_ref, w_out, r_out, x_v, xt, ub, rs, rb, rown, wt, wb, gacc, gx,
+        def kernel(x_hbm, w_hbm, y_hbm, eta_ref, out, x_v, xt, ub, rs, rb, rown, wt, wb, gacc, gx,
                    x_sem, in_sem, y_sem, rs_send, rs_recv, ag_send, ag_recv, gx_send, gx_recv):
+            w_out = out.at[:, pl.ds(rows, feat_len)]
+            r_out = out
             samp = lax.axis_index("samp")
             me = lax.axis_index("feat")
             cx, cy, cz = me % SIDE, (me // SIDE) % SIDE, me // (SIDE * SIDE)
@@ -136,9 +138,6 @@
                     src_ref=gacc.at[group], dst_ref=gx.at[group, slot], send_sem=gx_send.at[group],
                     recv_sem=gx_recv.at[group, slot], device_id=sibling, device_id_type=MESH_ID)
                 exchange.start()
-                sent = rs.at[pl.ds(0, feat_count - 1)]
-                wait_bytes(sent, rs_send.at[group])
-                wait_bytes(sent, ag_send.at[group])
                 exchange.wait_recv()
                 part = group_rows(group)
                 gradient = (gacc[group] + gx[group, slot]) * (1.0 / samples)
@@ -146,6 +145,9 @@
                 wt[part, :] = wt[part, :] + COMBINE_WEIGHT * delta
                 wb[part, :] = delta.astype(bf16)
                 exchange.wait_send()
+                sent = rs.at[pl.ds(0, feat_count - 1)]
+                wait_bytes(sent, rs_send.at[group])
+                wait_bytes(sent, ag_send.at[group])
 
             w_copy.wait()
             wb[...] = wt[...].astype(bf16)
@@ -205,9 +207,9 @@
         return pl.pallas_call(
             kernel,
             name="ridge_sweeps",
-            out_shape=(jax.ShapeDtypeStruct((targets, feat_len), f32), jax.ShapeDtypeStruct((targets, rows), f32)),
+            out_shape=jax.ShapeDtypeStruct((targets, rows + feat_len), f32),
             in_specs=[any_space, any_space, any_space, vmem],
-            out_specs=(any_space, any_space),
+            out_specs=any_space,
             scratch_shapes=[
                 pltpu.VMEM((rows, feat_len), bf16),
                 pltpu.VMEM((SIDE, feat_len, plane), bf16),
@@ -238,8 +240,8 @@
         samples = rows_loc * samp_count
         ridge = RIDGE_SCALE * (feat_len * feat_count) / samples
         call = make_kernel(rows_loc, feat_len, targets, ridge, samples)
-        weights, residual = call(x_loc, w_loc.T, y_loc.T, eta_loc.reshape(1, feat_len))
-        return weights.T, residual.T
+        both = call(x_loc, w_loc.T, y_loc.T, eta_loc.reshape(1, feat_len))
+        return both[:, rows_loc:].T, both[:, :rows_loc].T
 
     return jax.shard_map(
         local_solve,

time: 106 us -> 106 us (level)
    transpose x0 -> x2, local copies, waits for them, and re-layouts: none -> 3.94 us  [local_solve(): return (both[:, rows_loc:].T, both[:, :rows_loc].T)]
    unnamed x2 -> x0, local copies, waits for them, and re-layouts: 3.94 us -> none
where the time goes in v5:
time: 106 us
  Pallas kernels  101 us (95%)
  local copies, waits for them, and re-layouts  3.94 us (4%)
    pallas_call x1, Pallas kernels, local_solve(): both = call(x_loc, w_loc.T, y_loc.T, eta_loc.reshape(1, feat_len))  101 us
    transpose x2, local copies, waits for them, and re-layouts, local_solve(): return (both[:, rows_loc:].T, both[:, :rows_loc].T)  3.94 us

profile of v5, /device:TPU:1, one launch (start us, length us, event | category | flops | bytes accessed | tf_op | source)
XLA Modules:
  0.0 106.0 jit_solution(6555607178910574590)
XLA Ops:
  0.6 101.4 %ridge_sweeps.1 = f32[64,5120]{1,0:T(8,128)} custom-call(bf16[4096,1024]{1,0:T(8,128)(2,1)} %x_hbm.1, f32[64,1024]{1,0:T(8,128)} %bitcast.8, f32[64,4096]{1,0:T(8,128)} %bitcast.7, f32[1,1024]{1,0:T(1,128)} %bitcast.9), custom_call_target="tpu_custom_call" | custom-call | tf_op jit(solution)/shard_map/ridge_sweeps/pallas_call | solution.py:243
  102.0 1.7 %slice_bitcast_fusion.1 = f32[1024,64]{0,1:T(8,128)} fusion(f32[64,5120]{1,0:T(8,128)} %ridge_sweeps.1), kind=kLoop, calls=%fused_computation.1 | loop fusion | bytes 524288 | tf_op jit(solution)/shard_map/transpose | solution.py:244
  103.7 2.3 %slice_bitcast_fusion = f32[4096,64]{0,1:T(8,128)} fusion(f32[64,5120]{1,0:T(8,128)} %ridge_sweeps.1), kind=kLoop, calls=%fused_computation | loop fusion | bytes 2097152 | tf_op jit(solution)/shard_map/transpose | solution.py:244
